TPU v7x, 32 devices: a whole 2x2x4 slice. The times are simulated.
32 devices in a mesh: mem: 4 (over y, x), tile: 8 (over z, core).
Axes of the slice: x: 2, y: 2, z: 4, core: 2. Of those that a mesh axis runs over, the one named last changes fastest.
Arguments:
- ensemble: bfloat16 [8, 256, 64, 256], P('mem', None, 'tile'), may hold values from -4 to 4
- control: float32 [8, 64, 256], P('mem', 'tile'), may hold values from -6 to 6
- weights: float32 [8], P('mem'), may hold values from 0.1 to 0.6
- member_band: int32 [8], P('mem'), may hold values from 0 to 3
- spread: float32 [4], replicated, may hold values from 0.05 to 0.24
- advect: float32 [2, 256], replicated, may hold values from -0.9 to 0.9
- damping: float32 [256], replicated, may hold values from 0.02 to 0.2
- innovation: float32 [256, 64, 256], P(None, 'tile'), may hold values from -4 to 4
- obs_weight: float32 [64, 256], P('tile'), may hold values from 0.3 to 27
Outputs:
- grad_control: float32 [8, 64, 256], P('mem', 'tile')
- grad_weight: float32 [8], P('mem')
All inputs are finite; a program needn't handle non-finite values.
Results may differ from a plain program's by a relative error of at most 0.0003.
Values sent between devices are 32-bit elements; how exact they have to be, the bound alone decides.
A program may use at most 64 MiB of HBM per device.

v0:
```python
import math

import jax
import jax.numpy as jnp
from jax import lax
from jax.sharding import PartitionSpec as P

SWEEPS = 8


def extended_2(cells, sides, width):
    for axis, dim in sides:
        count = lax.axis_size(axis)
        head = lax.slice_in_dim(cells, 0, width, axis=dim)
        tail = lax.slice_in_dim(cells, cells.shape[dim] - width, cells.shape[dim], axis=dim)
        cells = jnp.concatenate(
            [
                lax.ppermute(tail, axis, [(i, (i + 1) % count) for i in range(count)]),
                cells,
                lax.ppermute(head, axis, [((i + 1) % count, i) for i in range(count)]),
            ],
            axis=dim,
        )
    return cells


def y_pairs(field):
    zero_col = jnp.zeros(field.shape[:-1] + (1,), field.dtype)
    north = jnp.concatenate([field[..., 1:], zero_col], axis=-1)
    south = jnp.concatenate([zero_col, field[..., :-1]], axis=-1)
    return (north, south)


def sweep_once(extended, rates):
    center = extended[:, 1:-1]
    east = extended[:, 2:]
    west = extended[:, :-2]
    north, south = y_pairs(center)
    return center + rates * (east + west + north + south - 4.0 * center)


def localize(field, rates):
    extended = extended_2(field, (("tile", 1),), SWEEPS)
    for sweep in range(SWEEPS):
        extended = sweep_once(extended, rates)
    return extended


def dynamics(field, along_x, along_y, smooth):
    extended = extended_2(field, (("tile", 1),), 1)
    center = extended[:, 1:-1]
    east = extended[:, 2:]
    west = extended[:, :-2]
    north, south = y_pairs(center)
    return (
        center
        - along_x * ((east - west) * 0.5)
        - along_y * ((north - south) * 0.5)
        + smooth * (east + west + north + south - 4.0 * center)
    )


def adjoint_gradient(increment, advect, damping, innovation, obs_weight):
    along_x = advect[0][:, None, None]
    along_y = advect[1][:, None, None]
    smooth = damping[:, None, None]
    forward = dynamics(increment, along_x, along_y, smooth)
    weighted = obs_weight[None] * (forward - innovation)
    return dynamics(weighted, -along_x, -along_y, smooth)


def per_device(
    ensemble, control, weights, member_band, spread, advect, damping, innovation, obs_weight
):
    one_hot = (
        member_band[:, None] == jnp.arange(spread.shape[0], dtype=jnp.int32)[None, :]
    ).astype(jnp.float32)
    rates = jnp.dot(one_hot, spread, precision=lax.Precision.HIGHEST)[:, None, None]
    localized = localize(control, rates)
    scaled = weights[:, None, None] * localized
    partial_value = jnp.sum(ensemble.astype(jnp.float32) * scaled[:, None], axis=0)
    increment = lax.psum(partial_value, "mem")
    gradient = adjoint_gradient(increment, advect, damping, innovation, obs_weight)
    projected = jnp.sum(ensemble.astype(jnp.float32) * gradient[None], axis=1)
    grad_control = control + localize(weights[:, None, None] * projected, rates)
    local_sums = jnp.sum(localized * projected, axis=(1, 2))
    total_cells = lax.axis_size("tile") * control.shape[1] * control.shape[2] * ensemble.shape[1]
    grad_weight = lax.psum(local_sums, "tile") / math.sqrt(total_cells)
    return (grad_control, grad_weight)


def solution(mesh):
    in_specs = (
        P("mem", None, "tile", None),
        P("mem", "tile", None),
        P("mem"),
        P("mem"),
        P(),
        P(),
        P(),
        P(None, "tile", None),
        P("tile", None),
    )
    out_specs = (P("mem", "tile", None), P("mem"))
    return jax.shard_map(
        per_device, mesh=mesh, in_specs=in_specs, out_specs=out_specs, check_vma=False
    )
```

profile of v0, /device:TPU:0, one launch (start us, length us, event | category | flops | bytes accessed | tf_op | source)
XLA Modules:
  0.0 146.0 jit_solution(15873035054924247474)
XLA Ops:
  7.2 4.6 %collective-permute-start.1 = (f32[2,8,256]{2,1,0:T(8,128)}, f32[2,8,256]{2,1,0:T(8,128)S(1)}, u32[]{:S(2)}, u32[]{:S(2)}) collective-permute-start(f32[2,8,256]{2,1,0:T(8,128)} %param.10), channel_id=1, source_target_pairs={{1,0},{2,1},{3,2},{4,3},{5,4},{6,5},{7,6},{0,7},{9,8},{10,9},{11,1... | collective-permute-start | bytes 49160 | tf_op jit(solution)/shard_map/ppermute | solution.py:20
  11.8 0.8 convolution_bitcast_fusion
  12.7 4.3 %collective-permute-done = f32[2,8,256]{2,1,0:T(8,128)S(1)} collective-permute-done((f32[2,8,256]{2,1,0:T(8,128)}, f32[2,8,256]{2,1,0:T(8,128)S(1)}, u32[]{:S(2)}, u32[]{:S(2)}) %collective-permute-start) | collective-permute-done | bytes 16416 | tf_op jit(solution)/shard_map/ppermute | solution.py:18
  17.0 0.7 constant_dynamic-update-slice_fusion.1
  18.0 0.1 fusion.26
  18.2 0.1 fusion.21
  19.1 1.8 %fusion = f32[256,8,256]{2,1,0:T(8,128)} fusion(bf16[2,256,8,256]{3,2,1,0:T(8,128)(2,1)S(1)} %copy-done.2, f32[2,8,256]{2,1,0:T(8,128)S(1)} %get-tuple-element.2), kind=kLoop, calls=%fused_computation.2 | loop fusion | flops 2621440 | bytes 4210688 | tf_op jit(solution)/shard_map/reduce_sum | solution.py:81
  20.9 0.7 copy-done.8
  21.6 67.2 %all-reduce.38.cloned.1.call-done = f32[256,8,256]{2,1,0:T(8,128)} async-done(((f32[256,8,256]{2,1,0:T(8,128)}), f32[256,8,256]{2,1,0:T(8,128)}) %all-reduce.38.cloned.1.call-update) | async-done | bytes 2097168 | tf_op jit(solution)/shard_map/psum | solution.py:82
  88.8 2.7 %fusion.90 = (f32[256,1,256]{2,1,0:T(1,128)S(1)}, f32[256,1,256]{2,1,0:T(1,128)S(1)}) fusion(f32[256,8,256]{2,1,0:T(8,128)} %all-reduce.38.cloned.1.call-done), kind=kLoop, calls=%fused_computation.126 | loop fusion | bytes 1048576 | tf_op jit(solution)/shard_map/slice | solution.py:15
  91.6 2.7 %collective-permute-start.2 = (f32[256,1,256]{2,0,1:T(8,128)S(1)}, f32[256,1,256]{2,0,1:T(8,128)S(1)}, u32[]{:S(2)}, u32[]{:S(2)}) collective-permute-start(f32[256,1,256]{2,0,1:T(8,128)S(1)} %copy.13), channel_id=1, source_target_pairs={{1,0},{2,1},{3,2},{4,3},{5,4},{6,5},{7,6},{0,7},{9,8},{10,9},{11,1... | collective-permute-start | bytes 786440 | tf_op jit(solution)/shard_map/ppermute | solution.py:20
  94.2 0.7 fusion.91
  94.9 4.4 %collective-permute-done.2 = f32[256,1,256]{2,0,1:T(8,128)S(1)} collective-permute-done((f32[256,1,256]{2,0,1:T(8,128)S(1)}, f32[256,1,256]{2,0,1:T(8,128)S(1)}, u32[]{:S(2)}, u32[]{:S(2)}) %collective-permute-start.2) | collective-permute-done | bytes 262176 | tf_op jit(solution)/shard_map/ppermute | solution.py:20
  99.3 0.3 copy.14
  99.6 2.5 %collective-permute-done.3 = f32[256,1,256]{2,0,1:T(8,128)S(1)} collective-permute-done((f32[256,1,256]{2,0,1:T(8,128)S(1)}, f32[256,1,256]{2,0,1:T(8,128)S(1)}, u32[]{:S(2)}, u32[]{:S(2)}) %collective-permute-start.3) | collective-permute-done | bytes 262176 | tf_op jit(solution)/shard_map/ppermute | solution.py:18
  102.1 0.3 copy.16
  102.4 2.9 %subtract_multiply_fusion = f32[256,8,256]{2,1,0:T(8,128)S(1)} fusion(f32[256,8,256]{2,1,0:T(8,128)S(1)} %copy-done.3, f32[256,8,256]{2,1,0:T(8,128)S(1)} %copy-done.1, f32[256,8,255]{2,1,0:T(8,128)S(1)} %get-tuple-element.11, f32[256,8,255]{2,1,0:T(8,128)S(1)} %get-tuple-element.10, f32[256,1,256]{2,1,0:T(1,128)S(1)} %copy.14, f32[256,1,256]{2,1,0:T(1,128)S(1)} %copy.16, ...), kind=kLoop, calls=%fused_computation.9 | loop fusion | flops 8912896 | bytes 11004928 | tf_op jit(solution)/shard_map/mul | solution.py:68
  105.3 0.3 fusion.88
  105.7 1.3 collective-permute-start.4
  106.9 0.7 fusion.89
  107.6 4.6 %collective-permute-done.4 = f32[256,1,256]{2,0,1:T(8,128)S(1)} collective-permute-done((f32[256,1,256]{2,0,1:T(8,128)S(1)}, f32[256,1,256]{2,0,1:T(8,128)S(1)}, u32[]{:S(2)}, u32[]{:S(2)}) %collective-permute-start.4) | collective-permute-done | bytes 262176 | tf_op jit(solution)/shard_map/ppermute | solution.py:20
  112.2 0.3 copy.18
  112.5 2.0 %collective-permute-done.5 = f32[256,1,256]{2,0,1:T(8,128)S(1)} collective-permute-done((f32[256,1,256]{2,0,1:T(8,128)S(1)}, f32[256,1,256]{2,0,1:T(8,128)S(1)}, u32[]{:S(2)}, u32[]{:S(2)}) %collective-permute-start.5) | collective-permute-done | bytes 262176 | tf_op jit(solution)/shard_map/ppermute | solution.py:18
  114.5 0.3 copy.20
  114.8 2.3 %multiply_add_fusion = f32[256,8,256]{2,1,0:T(8,128)S(1)} fusion(f32[256,8,256]{2,1,0:T(8,128)S(1)} %subtract_multiply_fusion, f32[256,8,255]{2,1,0:T(8,128)S(1)} %get-tuple-element.7, f32[256,8,255]{2,1,0:T(8,128)S(1)} %get-tuple-element.6, f32[256,1,256]{2,1,0:T(1,128)S(1)} %copy.18, f32[256,1,256]{2,1,0:T(1,128)S(1)} %copy.20, f32[256]{0:T(256)S(1)} %bitcast.12, ...), kind=kLoop, calls=%fused_computation.8 | loop fusion | flops 7864320 | bytes 8899584 | tf_op jit(solution)/shard_map/add | solution.py:56
  117.1 0.6 fusion.1
  117.7 0.1 multiply_reduce_fusion
  117.8 1.7 %collective-permute-start.7 = (f32[2,8,256]{2,1,0:T(8,128)S(1)}, f32[2,8,256]{2,1,0:T(8,128)S(1)}, u32[]{:S(2)}, u32[]{:S(2)}) collective-permute-start(f32[2,8,256]{2,1,0:T(8,128)S(1)} %get-tuple-element.45), channel_id=1, source_target_pairs={{1,0},{2,1},{3,2},{4,3},{5,4},{6,5},{7,6},{0,7},{9,8},{10,9},{11,1... | collective-permute-start | bytes 49160 | tf_op jit(solution)/shard_map/ppermute | solution.py:20
  119.5 17.1 %psum.15 = f32[2]{0:T(128)S(1)} all-reduce(f32[2]{0:T(128)S(1)} %get-tuple-element.44), channel_id=1, replica_groups=mesh['mem'=4,'tile'=8] {'tile'}, use_global_device_ids=true, to_apply=%region_4.0 | all-reduce | flops 2 | bytes 16 | tf_op jit(solution)/shard_map/psum | solution.py:88
  136.6 0.5 broadcast_multiply_fusion.2
  137.4 0.1 fusion.11
  138.5 0.7 fusion.77
  (62 shorter events, 2.5 us)
Async XLA Ops:
  7.2 4.7 %copy-start = (f32[4]{0:T(128)S(1)}, f32[4]{0:T(128)}, u32[]{:S(2)}) copy-start(f32[4]{0:T(128)} %param.13) | copy-start | bytes 52
  7.2 11.8 %copy-start.7 = (f32[2]{0:T(128)S(1)}, f32[2]{0:T(128)}, u32[]{:S(2)}) copy-start(f32[2]{0:T(128)} %param.11) | copy-start | bytes 28
  7.2 11.9 %copy-start.2 = (bf16[2,256,8,256]{3,2,1,0:T(8,128)(2,1)S(1)}, bf16[2,256,8,256]{3,2,1,0:T(8,128)(2,1)}, u32[]{:S(2)}) copy-start(bf16[2,256,8,256]{3,2,1,0:T(8,128)(2,1)} %param.9) | copy-start | bytes 6291460
  7.2 81.6 %all-reduce.38.cloned.1.call-start = ((), (), s32[]{:S(2)}) async-start(), calls=%async_computation | async-start | bytes 4194304 | tf_op jit(solution)/shard_map/psum | solution.py:82
  7.2 10.5 %collective-permute-start.1 = (f32[2,8,256]{2,1,0:T(8,128)}, f32[2,8,256]{2,1,0:T(8,128)S(1)}, u32[]{:S(2)}, u32[]{:S(2)}) collective-permute-start(f32[2,8,256]{2,1,0:T(8,128)} %param.10), channel_id=1, source_target_pairs={{1,0},{2,1},{3,2},{4,3},{5,4},{6,5},{7,6},{0,7},{9,8},{10,9},{11,1... | collective-permute-start | bytes 49160 | tf_op jit(solution)/shard_map/ppermute | solution.py:20
  11.8 5.2 %collective-permute-start = (f32[2,8,256]{2,1,0:T(8,128)}, f32[2,8,256]{2,1,0:T(8,128)S(1)}, u32[]{:S(2)}, u32[]{:S(2)}) collective-permute-start(f32[2,8,256]{2,1,0:T(8,128)} %param.10), channel_id=1, source_target_pairs={{0,1},{1,2},{2,3},{3,4},{4,5},{5,6},{6,7},{7,0},{8,9},{9,10},{10,1... | collective-permute-start | bytes 49160 | tf_op jit(solution)/shard_map/ppermute | solution.py:18
  20.9 0.7 copy-start.8
  88.8 5.5 %copy-start.1 = (f32[256,8,256]{2,1,0:T(8,128)S(1)}, f32[256,8,256]{2,1,0:T(8,128)}, u32[]{:S(2)}) copy-start(f32[256,8,256]{2,1,0:T(8,128)} %all-reduce.38.cloned.1.call-done) | copy-start | bytes 6291460
  91.5 10.8 %copy-start.5 = (f32[8,256]{1,0:T(8,128)S(1)}, f32[8,256]{1,0:T(8,128)}, u32[]{:S(2)}) copy-start(f32[8,256]{1,0:T(8,128)} %param.17) | copy-start | bytes 24580
  91.6 10.8 %copy-start.6 = (f32[256]{0:T(256)S(1)}, f32[256]{0:T(256)}, u32[]{:S(2)}) copy-start(f32[256]{0:T(256)} %param.15) | copy-start | bytes 3076
  91.6 7.7 %collective-permute-start.2 = (f32[256,1,256]{2,0,1:T(8,128)S(1)}, f32[256,1,256]{2,0,1:T(8,128)S(1)}, u32[]{:S(2)}, u32[]{:S(2)}) collective-permute-start(f32[256,1,256]{2,0,1:T(8,128)S(1)} %copy.13), channel_id=1, source_target_pairs={{1,0},{2,1},{3,2},{4,3},{5,4},{6,5},{7,6},{0,7},{9,8},{10,9},{11,1... | collective-permute-start | bytes 786440 | tf_op jit(solution)/shard_map/ppermute | solution.py:20
  94.2 7.9 %collective-permute-start.3 = (f32[256,1,256]{2,0,1:T(8,128)S(1)}, f32[256,1,256]{2,0,1:T(8,128)S(1)}, u32[]{:S(2)}, u32[]{:S(2)}) collective-permute-start(f32[256,1,256]{2,0,1:T(8,128)S(1)} %copy.15), channel_id=1, source_target_pairs={{0,1},{1,2},{2,3},{3,4},{4,5},{5,6},{6,7},{7,0},{8,9},{9,10},{10,1... | collective-permute-start | bytes 786440 | tf_op jit(solution)/shard_map/ppermute | solution.py:18
  94.2 8.2 %copy-start.3 = (f32[256,8,256]{2,1,0:T(8,128)S(1)}, f32[256,8,256]{2,1,0:T(8,128)}, u32[]{:S(2)}) copy-start(f32[256,8,256]{2,1,0:T(8,128)} %param.16) | copy-start | bytes 6291460
  105.7 6.6 %collective-permute-start.4 = (f32[256,1,256]{2,0,1:T(8,128)S(1)}, f32[256,1,256]{2,0,1:T(8,128)S(1)}, u32[]{:S(2)}, u32[]{:S(2)}) collective-permute-start(f32[256,1,256]{2,0,1:T(8,128)S(1)} %copy.17), channel_id=1, source_target_pairs={{1,0},{2,1},{3,2},{4,3},{5,4},{6,5},{7,6},{0,7},{9,8},{10,9},{11,1... | collective-permute-start | bytes 786440 | tf_op jit(solution)/shard_map/ppermute | solution.py:20
  106.9 7.6 %collective-permute-start.5 = (f32[256,1,256]{2,0,1:T(8,128)S(1)}, f32[256,1,256]{2,0,1:T(8,128)S(1)}, u32[]{:S(2)}, u32[]{:S(2)}) collective-permute-start(f32[256,1,256]{2,0,1:T(8,128)S(1)} %copy.19), channel_id=1, source_target_pairs={{0,1},{1,2},{2,3},{3,4},{4,5},{5,6},{6,7},{7,0},{8,9},{9,10},{10,1... | collective-permute-start | bytes 786440 | tf_op jit(solution)/shard_map/ppermute | solution.py:18
  117.7 20.8 %copy-start.4 = (f32[2,8,256]{2,1,0:T(8,128)S(1)}, f32[2,8,256]{2,1,0:T(8,128)}, u32[]{:S(2)}) copy-start(f32[2,8,256]{2,1,0:T(8,128)} %param.10) | copy-start | bytes 49156
  117.8 19.4 %collective-permute-start.7 = (f32[2,8,256]{2,1,0:T(8,128)S(1)}, f32[2,8,256]{2,1,0:T(8,128)S(1)}, u32[]{:S(2)}, u32[]{:S(2)}) collective-permute-start(f32[2,8,256]{2,1,0:T(8,128)S(1)} %get-tuple-element.45), channel_id=1, source_target_pairs={{1,0},{2,1},{3,2},{4,3},{5,4},{6,5},{7,6},{0,7},{9,8},{10,9},{11,1... | collective-permute-start | bytes 49160 | tf_op jit(solution)/shard_map/ppermute | solution.py:20
  119.5 17.7 %collective-permute-start.6 = (f32[2,8,256]{2,1,0:T(8,128)S(1)}, f32[2,8,256]{2,1,0:T(8,128)S(1)}, u32[]{:S(2)}, u32[]{:S(2)}) collective-permute-start(f32[2,8,256]{2,1,0:T(8,128)S(1)} %get-tuple-element.45), channel_id=1, source_target_pairs={{0,1},{1,2},{2,3},{3,4},{4,5},{5,6},{6,7},{7,0},{8,9},{9,10},{10,1... | collective-permute-start | bytes 49160 | tf_op jit(solution)/shard_map/ppermute | solution.py:18
Sparse Core Ops, SparseCore 0:
  21.0 67.6 all-reduce.37
where the time goes:
time: 146 us
  waiting for transfers between devices  85.1 us (58%)
  blocking collectives  17.1 us (12%)
  between operations  14.3 us (10%)
  starting transfers between devices  10.2 us (7%)
  other arithmetic  10.2 us (7%)
  local copies, waits for them, and re-layouts  8.25 us (6%)
    psum x1, waiting for transfers between devices, per_device(): increment = lax.psum(partial_value, 'mem')  67.2 us
    psum x1, blocking collectives, per_device(): grad_weight = lax.psum(local_sums, 'tile') / math.sqrt(total_cells)  17.1 us
    ppermute x4, starting transfers between devices, extended_2(): lax.ppermute(head, axis, [((i + 1) % count, i) for i in range(count)])  10.2 us
    ppermute x4, waiting for transfers between devices, extended_2(): lax.ppermute(head, axis, [((i + 1) % count, i) for i in range(count)])  8.98 us
    ppermute x4, waiting for transfers between devices, extended_2(): lax.ppermute(tail, axis, [(i, (i + 1) % count) for i in range(count)])  8.9 us
    slice x4, local copies, waits for them, and re-layouts, extended_2(): lax.slice_in_dim(cells, cells.shape[dim] - width, cells.shape[dim], axis=...  3.09 us
  transfers between devices with their start and end apart: 9, of which 6 were waited for; matrix products, arithmetic and copies ran while one was open for 3% of the time, Pallas kernels for 0%

commit v1 on v0

v1 whole, which is shorter than its diff:
```python
import functools
import math

import jax
import jax.numpy as jnp
from jax import lax
from jax.experimental import pallas as pl
from jax.experimental.pallas import tpu as pltpu
from jax.sharding import PartitionSpec as P

SWEEPS = 8
STEPS = 8
LAG_C = 2
LAG_D = 4
LAG_E = 6
LAG_F = 7
MESH = pl.DeviceIdType.MESH


def factors(n):
    a = max(d for d in range(1, n + 1) if n % d == 0 and d * d <= n)
    return a, n // a


def y_pair(f):
    ny = f.shape[-1]
    col = lax.broadcasted_iota(jnp.int32, f.shape, 1)
    north = jnp.where(col == ny - 1, 0.0, pltpu.roll(f, ny - 1, 1))
    south = jnp.where(col == 0, 0.0, pltpu.roll(f, 1, 1))
    return north, south


def stencil(f, a, b, e):
    rows = f.shape[0]
    north, south = y_pair(f)
    east = pltpu.roll(f, rows - 1, 0)
    west = pltpu.roll(f, 1, 0)
    return (
        (1.0 - 4.0 * e) * f
        + (e - 0.5 * a) * east
        + (e + 0.5 * a) * west
        + (e - 0.5 * b) * north
        + (e + 0.5 * b) * south
    )


def sweeps(f, rates):
    rows = f.shape[0]
    for _ in range(SWEEPS):
        north, south = y_pair(f)
        east = pltpu.roll(f, rows - 1, 0)
        west = pltpu.roll(f, 1, 0)
        f = f + rates * (east + west + north + south - 4.0 * f)
    return f


def kernel(
    n, tiles, steps, planes,
    ens, control, weights, band, spread, advect, damping, innov, obs,
    out, gw_out,
    e_v, iv, loc, scl, proj, own, part, grad, r1a, r1b, r2a, r2b,
    ch, wh, ih, hh, ph, gwr,
    e_sem, i_sem,
    s1s, s1r, s2s, s2r, s3s, s3r, s4s, s4r,
    hs, hr, xs, xr, gs, gr,
):
    a, b = factors(n)
    ml = control.shape[0]
    rows = control.shape[1]
    me = lax.axis_index("mem")
    t = lax.axis_index("tile")
    ia = me // b
    ib = me % b
    nxt = (t + 1) % tiles
    prv = (t + tiles - 1) % tiles
    r1 = (r1a, r1b)
    r2 = (r2a, r2b)
    first = (b, a)
    second = (a, b)
    fi = (ib, ia)
    gi = (ia, ib)

    def device(q, f, g):
        return g * b + f if q == 0 else f * b + g

    def plane0(s, q):
        return (s * 2 + q) * (n * planes)

    def mine(q):
        return (fi[q] * second[q] + gi[q]) * planes

    for m in range(ml):
        pltpu.make_async_copy(ens.at[m], e_v.at[m], e_sem.at[m]).start()

    def innov_copy(s, q):
        return pltpu.make_async_copy(
            innov.at[pl.ds(plane0(s, q) + mine(q), planes)],
            iv.at[pl.ds((s * 2 + q) * planes, planes)],
            i_sem.at[s, q],
        )

    @pl.loop(0, steps)
    def _(s):
        for q in range(2):
            innov_copy(s, q).start()

    barrier = pltpu.get_barrier_semaphore()
    for d in range(1, tiles):
        pl.semaphore_signal(
            barrier, inc=1, device_id={"tile": (t + d) % tiles}, device_id_type=MESH
        )
    for d in range(1, b):
        pl.semaphore_signal(
            barrier, inc=1, device_id={"mem": device(0, (ib + d) % b, ia)}, device_id_type=MESH
        )
    for d in range(1, a):
        pl.semaphore_signal(
            barrier, inc=1, device_id={"mem": device(0, ib, (ia + d) % a)}, device_id_type=MESH
        )
    pl.semaphore_wait(barrier, tiles - 1 + a - 1 + b - 1)

    def to_tile(src, dst, k, dev):
        return pltpu.make_async_remote_copy(
            src_ref=src, dst_ref=dst, send_sem=xs.at[k], recv_sem=xr.at[k],
            device_id={"tile": dev}, device_id_type=MESH,
        )

    def both(src, dst, k):
        return (
            to_tile(src, dst.at[0], k, nxt),
            to_tile(src, dst.at[1], k + 1, prv),
        )

    c_copy = both(control, ch, 0)
    w_copy = both(obs, wh, 2)
    i_copy = both(iv, ih, 4)
    p_copy = both(scl, ph, 6)
    for c in c_copy + w_copy:
        c.start()

    rate_rows = []
    for m in range(ml):
        rate_rows.append(
            jnp.full((3 * rows, control.shape[2]), spread[band[m]], jnp.float32)
        )
    rates = jnp.concatenate(rate_rows, axis=0)
    for c in c_copy:
        c.wait_recv()
    field = []
    for m in range(ml):
        field += [ch[0, m], control[m], ch[1, m]]
    field = sweeps(jnp.concatenate(field, axis=0), rates)
    for m in range(ml):
        center = field[(3 * m + 1) * rows : (3 * m + 2) * rows]
        loc[m] = center
        scl[m] = weights[m] * center
        proj[m] = jnp.zeros_like(center)
    for m in range(ml):
        pltpu.make_async_copy(ens.at[m], e_v.at[m], e_sem.at[m]).wait()

    def stage1(s, q, d):
        f, g = first[q], second[q]
        to = (fi[q] + d) % f
        return pltpu.make_async_remote_copy(
            src_ref=part.at[s, q, pl.ds(to * (g * planes), g * planes)],
            dst_ref=r1[q].at[s, d - 1],
            send_sem=s1s.at[s, q, d - 1], recv_sem=s1r.at[s, q, d - 1],
            device_id={"mem": device(q, to, gi[q])}, device_id_type=MESH,
        )

    def stage2(s, q, d):
        g = second[q]
        to = (gi[q] + d) % g
        return pltpu.make_async_remote_copy(
            src_ref=part.at[s, q, pl.ds((fi[q] * g + to) * planes, planes)],
            dst_ref=r2[q].at[s, d - 1],
            send_sem=s2s.at[s, q, d - 1], recv_sem=s2r.at[s, q, d - 1],
            device_id={"mem": device(q, fi[q], to)}, device_id_type=MESH,
        )

    def stage3(s, q, d, incoming=False):
        g = second[q]
        to = (gi[q] + d) % g
        where = (gi[q] + g - d) % g if incoming else gi[q]
        block = grad.at[s, q, pl.ds((fi[q] * g + where) * planes, planes)]
        return pltpu.make_async_remote_copy(
            src_ref=block, dst_ref=block,
            send_sem=s3s.at[s, q, d - 1], recv_sem=s3r.at[s, q, d - 1],
            device_id={"mem": device(q, fi[q], to)}, device_id_type=MESH,
        )

    def stage4(s, q, d, incoming=False):
        f, g = first[q], second[q]
        to = (fi[q] + d) % f
        where = (fi[q] + f - d) % f if incoming else fi[q]
        block = grad.at[s, q, pl.ds(where * (g * planes), g * planes)]
        return pltpu.make_async_remote_copy(
            src_ref=block, dst_ref=block,
            send_sem=s4s.at[s, q, d - 1], recv_sem=s4r.at[s, q, d - 1],
            device_id={"mem": device(q, to, gi[q])}, device_id_type=MESH,
        )

    def halo(s):
        return tuple(
            pltpu.make_async_remote_copy(
                src_ref=own.at[s], dst_ref=hh.at[way, s],
                send_sem=hs.at[way, s], recv_sem=hr.at[way, s],
                device_id={"tile": dev}, device_id_type=MESH,
            )
            for way, dev in enumerate((nxt, prv))
        )

    def part_of(s):
        for q in range(2):
            total = None
            for m in range(ml):
                term = e_v[m, pl.ds(plane0(s, q), n * planes)].astype(jnp.float32) * scl[m][None]
                total = term if total is None else total + term
            part[s, q] = total
        for q in range(2):
            for d in range(1, first[q]):
                stage1(s, q, d).start()

    def reduce_first(s):
        for q in range(2):
            g = second[q]
            for d in range(1, first[q]):
                stage1(s, q, d).wait_recv()
            block = pl.ds(fi[q] * (g * planes), g * planes)
            total = part[s, q, block]
            for d in range(1, first[q]):
                total = total + r1[q][s, d - 1]
            part[s, q, block] = total
        for q in range(2):
            for d in range(1, second[q]):
                stage2(s, q, d).start()

    def reduce_second(s):
        for q in range(2):
            for d in range(1, second[q]):
                stage2(s, q, d).wait_recv()
            total = part[s, q, pl.ds(mine(q), planes)]
            for d in range(1, second[q]):
                total = total + r2[q][s, d - 1]
            own[s, q * planes : (q + 1) * planes] = total
        for c in halo(s):
            c.start()

    def adjoint(s):
        for c in halo(s):
            c.wait_recv()
        weight = jnp.concatenate([wh[0], obs[...], wh[1]], axis=0)
        for q in range(2):
            for p in range(planes):
                k = plane0(s, q) + mine(q) + p
                ax = advect[0, k]
                ay = advect[1, k]
                e = damping[k]
                i = q * planes + p
                j = s * (2 * planes) + i
                f = jnp.concatenate([hh[0, s, i], own[s, i], hh[1, s, i]], axis=0)
                o = jnp.concatenate([ih[0, j], iv[j], ih[1, j]], axis=0)
                w = weight * (stencil(f, ax, ay, e) - o)
                grad[s, q, mine(q) + p] = stencil(w, -ax, -ay, e)[rows : 2 * rows]
        for q in range(2):
            for d in range(1, second[q]):
                stage3(s, q, d).start()

    def spread_grad(s):
        for q in range(2):
            for d in range(1, second[q]):
                stage3(s, q, d, True).wait_recv()
        for q in range(2):
            for d in range(1, first[q]):
                stage4(s, q, d).start()

    def project(s):
        for q in range(2):
            for d in range(1, first[q]):
                stage4(s, q, d, True).wait_recv()
        for q in range(2):
            g = grad[s, q]
            for m in range(ml):
                e = e_v[m, pl.ds(plane0(s, q), n * planes)].astype(jnp.float32)
                proj[m] += jnp.sum(e * g, axis=0)

    @pl.loop(0, steps)
    def _(s):
        part_of(s)

    @pl.loop(0, steps)
    def _(s):
        for q in range(2):
            innov_copy(s, q).wait()

    for c in i_copy:
        c.start()
    for c in w_copy + i_copy:
        c.wait_recv()

    @pl.loop(0, steps + LAG_F)
    def _(tick):
        for lag, stage in (
            (0, reduce_first),
            (LAG_C, reduce_second),
            (LAG_D, adjoint),
            (LAG_E, spread_grad),
            (LAG_F, project),
        ):
            @pl.when(jnp.logical_and(tick >= lag, tick < steps + lag))
            def _(lag=lag, stage=stage):
                stage(tick - lag)

    for m in range(ml):
        scl[m] = weights[m] * proj[m]
    row = lax.broadcasted_iota(jnp.int32, (8, 128), 0)
    sums = jnp.zeros((8, 128), jnp.float32)
    for m in range(ml):
        v = jnp.sum(loc[m] * proj[m], axis=0, keepdims=True)
        v = sum(v[:, c : c + 128] for c in range(0, v.shape[1], 128))
        sums = jnp.where(row == m, jnp.broadcast_to(v, (8, 128)), sums)
    gwr[t] = sums
    for c in p_copy:
        c.start()

    def gw_copy(d, incoming=False):
        slot = (t + tiles - d) % tiles if incoming else t
        return pltpu.make_async_remote_copy(
            src_ref=gwr.at[slot], dst_ref=gwr.at[slot],
            send_sem=gs.at[d - 1], recv_sem=gr.at[d - 1],
            device_id={"tile": (t + d) % tiles}, device_id_type=MESH,
        )

    for d in range(1, tiles):
        gw_copy(d).start()
    for c in p_copy:
        c.wait_recv()
    field = []
    for m in range(ml):
        field += [ph[0, m], scl[m], ph[1, m]]
    field = sweeps(jnp.concatenate(field, axis=0), rates)
    for m in range(ml):
        out[m] = control[m] + field[(3 * m + 1) * rows : (3 * m + 2) * rows]
    for d in range(1, tiles):
        gw_copy(d, True).wait_recv()
    total = gwr[0]
    for d in range(1, tiles):
        total = total + gwr[d]
    gw_out[...] = jnp.broadcast_to(jnp.sum(total, axis=1, keepdims=True), (8, 128))

    for c in c_copy + w_copy + i_copy + p_copy:
        c.wait_send()
    for d in range(1, tiles):
        gw_copy(d).wait_send()

    @pl.loop(0, steps)
    def _(s):
        for c in halo(s):
            c.wait_send()
        for q in range(2):
            for d in range(1, first[q]):
                stage1(s, q, d).wait_send()
                stage4(s, q, d).wait_send()
            for d in range(1, second[q]):
                stage2(s, q, d).wait_send()
                stage3(s, q, d).wait_send()


def per_device(
    n, tiles,
    ensemble, control, weights, member_band, spread, advect, damping, innovation, obs_weight
):
    ml, vl, rows, ny = ensemble.shape
    assert rows == SWEEPS and ny % 128 == 0 and ml <= 8 and vl % (2 * n) == 0
    steps = max(d for d in range(1, STEPS + 1) if (vl // (2 * n)) % d == 0)
    planes = vl // (2 * n * steps)
    a, b = factors(n)
    f32 = jnp.float32
    peers = max(a, b, 2) - 1
    dma = pltpu.SemaphoreType.DMA
    vmem = pl.BlockSpec(memory_space=pltpu.VMEM)
    smem = pl.BlockSpec(memory_space=pltpu.SMEM)
    hbm = pl.BlockSpec(memory_space=pl.ANY)
    field = (rows, ny)
    out, gw = pl.pallas_call(
        functools.partial(kernel, n, tiles, steps, planes),
        out_shape=(
            jax.ShapeDtypeStruct((ml, rows, ny), f32),
            jax.ShapeDtypeStruct((8, 128), f32),
        ),
        in_specs=[hbm, vmem, smem, smem, smem, smem, smem, hbm, vmem],
        out_specs=(vmem, vmem),
        scratch_shapes=[
            pltpu.VMEM((ml, vl) + field, ensemble.dtype),
            pltpu.VMEM((steps * 2 * planes,) + field, f32),
            pltpu.VMEM((ml,) + field, f32),
            pltpu.VMEM((ml,) + field, f32),
            pltpu.VMEM((ml,) + field, f32),
            pltpu.VMEM((steps, 2 * planes) + field, f32),
            pltpu.VMEM((steps, 2, n * planes) + field, f32),
            pltpu.VMEM((steps, 2, n * planes) + field, f32),
            pltpu.VMEM((steps, max(b - 1, 1), a * planes) + field, f32),
            pltpu.VMEM((steps, max(a - 1, 1), b * planes) + field, f32),
            pltpu.VMEM((steps, max(a - 1, 1), planes) + field, f32),
            pltpu.VMEM((steps, max(b - 1, 1), planes) + field, f32),
            pltpu.VMEM((2, ml) + field, f32),
            pltpu.VMEM((2,) + field, f32),
            pltpu.VMEM((2, steps * 2 * planes) + field, f32),
            pltpu.VMEM((2, steps, 2 * planes) + field, f32),
            pltpu.VMEM((2, ml) + field, f32),
            pltpu.VMEM((tiles, 8, 128), f32),
            dma((ml,)),
            dma((steps, 2)),
        ]
        + [dma((steps, 2, peers))] * 8
        + [dma((2, steps))] * 2
        + [dma((8,))] * 2
        + [dma((tiles - 1,))] * 2,
        compiler_params=pltpu.CompilerParams(
            collective_id=0, has_side_effects=True, vmem_limit_bytes=60 * 1024 * 1024
        ),
    )(ensemble, control, weights, member_band, spread, advect, damping, innovation, obs_weight)
    total_cells = tiles * rows * ny * vl
    return out, gw[:ml, 0] / math.sqrt(total_cells)


def solution(mesh):
    in_specs = (
        P("mem", None, "tile", None),
        P("mem", "tile", None),
        P("mem"),
        P("mem"),
        P(),
        P(),
        P(),
        P(None, "tile", None),
        P("tile", None),
    )
    out_specs = (P("mem", "tile", None), P("mem"))
    return jax.shard_map(
        functools.partial(per_device, mesh.shape["mem"], mesh.shape["tile"]),
        mesh=mesh, in_specs=in_specs, out_specs=out_specs, check_vma=False,
    )
```

time: 146 us -> 61.3 us (0.42)
  waiting for transfers between devices: 85.1 us -> 0 us
  Pallas kernels: 0 us -> 57.8 us
  blocking collectives: 17.1 us -> 0 us
  between operations: 14.3 us -> 0.64 us
  starting transfers between devices: 10.2 us -> 0 us
  other arithmetic: 10.2 us -> 1.3 us
  local copies, waits for them, and re-layouts: 8.25 us -> 1.32 us
    psum x1 -> x0, waiting for transfers between devices: 67.2 us -> none  [per_device(): increment = lax.psum(partial_value, 'mem')]
    pallas_call x0 -> x1, Pallas kernels: none -> 57.8 us  [per_device(): pl.pallas_call(functools.partial(kernel, n, tiles, steps, planes), out_sh...]
    ppermute x8 -> x0, waiting for transfers between devices: 17.9 us -> none  [the longest x4 8.98 us: extended_2(): lax.ppermute(head, axis, [((i + 1) % count, i) for i in range(count)])]
    psum x1 -> x0, blocking collectives: 17.1 us -> none  [per_device(): grad_weight = lax.psum(local_sums, 'tile') / math.sqrt(total_cells)]
    ppermute x8 -> x0, starting transfers between devices: 10.2 us -> none  [the longest x4 10.2 us: extended_2(): lax.ppermute(head, axis, [((i + 1) % count, i) for i in range(count)])]
    slice x24 -> x0, local copies, waits for them, and re-layouts: 5.74 us -> none  [the longest x4 3.09 us: extended_2(): lax.slice_in_dim(cells, cells.shape[dim] - width, cells.shape[dim], axis=...]
    add x16 -> x0, other arithmetic: 4.23 us -> none  [the longest x1 2.32 us: dynamics(): center - along_x * ((east - west) * 0.5) - along_y * ((north - south) * 0.5)]
    mul x3 -> x0, other arithmetic: 2.94 us -> none  [the longest x1 2.85 us: adjoint_gradient(): weighted = obs_weight[None] * (forward - innovation)]
  transfers between devices with their start and end apart: 9 -> 0, of which waited for: 6 -> 0; matrix products, arithmetic and copies ran while one was open for 3% -> 0% of each run, Pallas kernels for 0% -> 0%
where the time goes in v1:
time: 61.3 us; the launch traced here: 61.1 us
  Pallas kernels  57.8 us (94%)
  local copies, waits for them, and re-layouts  1.32 us (2%)
  other arithmetic  1.3 us (2%)
  between operations  0.64 us (1%)
    pallas_call x1, Pallas kernels, per_device(): pl.pallas_call(functools.partial(kernel, n, tiles, steps, planes), out_sh...  57.8 us
    unnamed x1, local copies, waits for them, and re-layouts  1.32 us
    div x1, other arithmetic, per_device(): return (out, gw[:ml, 0] / math.sqrt(total_cells))  1.3 us

profile of v1, /device:TPU:0, one launch (start us, length us, event | category | flops | bytes accessed | tf_op | source)
XLA Modules:
  0.0 61.1 jit_solution(16872363144999500993)
XLA Ops:
  0.6 57.8 %shard_map.104 = (f32[2,8,256]{2,1,0:T(8,128)}, f32[8,128]{1,0:T(8,128)}) custom-call(bf16[2,256,8,256]{3,2,1,0:T(8,128)(2,1)} %ens.1, f32[2,8,256]{2,1,0:T(8,128)} %control.1, f32[2]{0:T(128)} %weights.1, s32[2]{0:T(128)} %band.1, f32[4]{0:T(128)} %spread.1, f32[2,256]{1,0:T(2,128)} %advect.1, f32[256]{0:T(256)} %damping.1, f32[256,8,256]{2,1,0:T(8,128)} %innov.1, ...), custom_call_target="tpu_custom_call" | custom-call | tf_op jit(solution)/shard_map/pallas_call | solution.py:385
  58.4 1.3 %multiply_reduce_fusion = f32[2]{0:T(128)} fusion(f32[8,128]{1,0:T(8,128)} %get-tuple-element.5), kind=kLoop, calls=%fused_computation | loop fusion | flops 2 | bytes 16 | tf_op jit(solution)/shard_map/div | solution.py:424
  59.7 1.3 %copy.12 = f32[2,8,256]{2,1,0:T(8,128)} copy(f32[2,8,256]{2,1,0:T(8,128)} %get-tuple-element.8) | data formatting | bytes 32768

commit v2 on v1

--- a/solution.py
+++ b/solution.py
@@ -133,9 +133,20 @@
 
     c_copy = both(control, ch, 0)
     w_copy = both(obs, wh, 2)
-    i_copy = both(iv, ih, 4)
+    i_copy = (
+        to_tile(iv.at[:, rows - 1 :, :], ih.at[0, :, rows - 1 :, :], 4, nxt),
+        to_tile(iv.at[:, :1, :], ih.at[1, :, :1, :], 5, prv),
+    )
     p_copy = both(scl, ph, 6)
     for c in c_copy + w_copy:
+        c.start()
+
+    @pl.loop(0, steps)
+    def _(s):
+        for q in range(2):
+            innov_copy(s, q).wait()
+
+    for c in i_copy:
         c.start()
 
     rate_rows = []
@@ -203,11 +214,13 @@
     def halo(s):
         return tuple(
             pltpu.make_async_remote_copy(
-                src_ref=own.at[s], dst_ref=hh.at[way, s],
+                src_ref=own.at[s, :, edge, :], dst_ref=hh.at[way, s, :, edge, :],
                 send_sem=hs.at[way, s], recv_sem=hr.at[way, s],
                 device_id={"tile": dev}, device_id_type=MESH,
             )
-            for way, dev in enumerate((nxt, prv))
+            for way, (dev, edge) in enumerate(
+                ((nxt, slice(rows - 2, rows)), (prv, slice(0, 2)))
+            )
         )
 
     def part_of(s):
@@ -288,18 +301,13 @@
     def _(s):
         part_of(s)
 
-    @pl.loop(0, steps)
-    def _(s):
-        for q in range(2):
-            innov_copy(s, q).wait()
-
-    for c in i_copy:
-        c.start()
-    for c in w_copy + i_copy:
-        c.wait_recv()
-
     @pl.loop(0, steps + LAG_F)
     def _(tick):
+        @pl.when(tick == LAG_D)
+        def _():
+            for c in w_copy + i_copy:
+                c.wait_recv()
+
         for lag, stage in (
             (0, reduce_first),
             (LAG_C, reduce_second),

time: 61.3 us -> 58.5 us (0.954)
  Pallas kernels: 57.8 us -> 55 us
    pallas_call x1, Pallas kernels: 57.8 us -> 55 us  [per_device(): pl.pallas_call(functools.partial(kernel, n, tiles, steps, planes), out_sh...]
where the time goes in v2:
time: 58.5 us; the launch traced here: 58.2 us
  Pallas kernels  55 us (94%)
  local copies, waits for them, and re-layouts  1.32 us (2%)
  other arithmetic  1.3 us (2%)
  between operations  0.64 us (1%)
    pallas_call x1, Pallas kernels, per_device(): pl.pallas_call(functools.partial(kernel, n, tiles, steps, planes), out_sh...  55 us
    unnamed x1, local copies, waits for them, and re-layouts  1.32 us
    div x1, other arithmetic, per_device(): return (out, gw[:ml, 0] / math.sqrt(total_cells))  1.3 us

profile of v2, /device:TPU:0, one launch (start us, length us, event | category | flops | bytes accessed | tf_op | source)
XLA Modules:
  0.0 58.2 jit_solution(7579765207001529160)
XLA Ops:
  0.6 55.0 %shard_map.104 = (f32[2,8,256]{2,1,0:T(8,128)}, f32[8,128]{1,0:T(8,128)}) custom-call(bf16[2,256,8,256]{3,2,1,0:T(8,128)(2,1)} %ens.1, f32[2,8,256]{2,1,0:T(8,128)} %control.1, f32[2]{0:T(128)} %weights.1, s32[2]{0:T(128)} %band.1, f32[4]{0:T(128)} %spread.1, f32[2,256]{1,0:T(2,128)} %advect.1, f32[256]{0:T(256)} %damping.1, f32[256,8,256]{2,1,0:T(8,128)} %innov.1, ...), custom_call_target="tpu_custom_call" | custom-call | tf_op jit(solution)/shard_map/pallas_call | solution.py:393
  55.6 1.3 %multiply_reduce_fusion = f32[2]{0:T(128)} fusion(f32[8,128]{1,0:T(8,128)} %get-tuple-element.5), kind=kLoop, calls=%fused_computation | loop fusion | flops 2 | bytes 16 | tf_op jit(solution)/shard_map/div | solution.py:432
  56.9 1.3 %copy.12 = f32[2,8,256]{2,1,0:T(8,128)} copy(f32[2,8,256]{2,1,0:T(8,128)} %get-tuple-element.8) | data formatting | bytes 32768

commit v3 on v2

--- a/solution.py
+++ b/solution.py
@@ -9,11 +9,11 @@
 from jax.sharding import PartitionSpec as P
 
 SWEEPS = 8
-STEPS = 8
+STEPS = 4
 LAG_C = 2
-LAG_D = 4
-LAG_E = 6
-LAG_F = 7
+LAG_D = 3
+LAG_E = 4
+LAG_F = 5
 MESH = pl.DeviceIdType.MESH
 
 
@@ -56,8 +56,9 @@
 
 def kernel(
     n, tiles, steps, planes,
-    ens, control, weights, band, spread, advect, damping, innov, obs,
-    out, gw_out,
+    ens, control_h, weights_h, band_h, spread_h, advect_h, damping_h, innov, obs_h,
+    out_h, gw_h,
+    control, weights, band, spread, advect, damping, obs, out, gw_out, arg_sem, out_sem,
     e_v, iv, loc, scl, proj, own, part, grad, r1a, r1b, r2a, r2b,
     ch, wh, ih, hh, ph, gwr,
     e_sem, i_sem,
@@ -89,8 +90,15 @@
     def mine(q):
         return (fi[q] * second[q] + gi[q]) * planes
 
-    for m in range(ml):
-        pltpu.make_async_copy(ens.at[m], e_v.at[m], e_sem.at[m]).start()
+    args = [
+        pltpu.make_async_copy(src, dst, arg_sem.at[i])
+        for i, (src, dst) in enumerate((
+            (control_h, control), (obs_h, obs), (weights_h, weights), (band_h, band),
+            (spread_h, spread), (advect_h, advect), (damping_h, damping),
+        ))
+    ]
+    for c in args:
+        c.start()
 
     def innov_copy(s, q):
         return pltpu.make_async_copy(
@@ -103,6 +111,9 @@
     def _(s):
         for q in range(2):
             innov_copy(s, q).start()
+
+    for m in range(ml):
+        pltpu.make_async_copy(ens.at[m], e_v.at[m], e_sem.at[m]).start()
 
     barrier = pltpu.get_barrier_semaphore()
     for d in range(1, tiles):
@@ -138,8 +149,12 @@
         to_tile(iv.at[:, :1, :], ih.at[1, :, :1, :], 5, prv),
     )
     p_copy = both(scl, ph, 6)
+    for c in args[:2]:
+        c.wait()
     for c in c_copy + w_copy:
         c.start()
+    for c in args[2:]:
+        c.wait()
 
     @pl.loop(0, steps)
     def _(s):
@@ -349,12 +364,18 @@
     field = sweeps(jnp.concatenate(field, axis=0), rates)
     for m in range(ml):
         out[m] = control[m] + field[(3 * m + 1) * rows : (3 * m + 2) * rows]
+    outs = (
+        pltpu.make_async_copy(out, out_h, out_sem.at[0]),
+        pltpu.make_async_copy(gw_out, gw_h, out_sem.at[1]),
+    )
+    outs[0].start()
     for d in range(1, tiles):
         gw_copy(d, True).wait_recv()
     total = gwr[0]
     for d in range(1, tiles):
         total = total + gwr[d]
     gw_out[...] = jnp.broadcast_to(jnp.sum(total, axis=1, keepdims=True), (8, 128))
+    outs[1].start()
 
     for c in c_copy + w_copy + i_copy + p_copy:
         c.wait_send()
@@ -372,6 +393,8 @@
             for d in range(1, second[q]):
                 stage2(s, q, d).wait_send()
                 stage3(s, q, d).wait_send()
+    for c in outs:
+        c.wait()
 
 
 def per_device(
@@ -386,8 +409,6 @@
     f32 = jnp.float32
     peers = max(a, b, 2) - 1
     dma = pltpu.SemaphoreType.DMA
-    vmem = pl.BlockSpec(memory_space=pltpu.VMEM)
-    smem = pl.BlockSpec(memory_space=pltpu.SMEM)
     hbm = pl.BlockSpec(memory_space=pl.ANY)
     field = (rows, ny)
     out, gw = pl.pallas_call(
@@ -396,9 +417,20 @@
             jax.ShapeDtypeStruct((ml, rows, ny), f32),
             jax.ShapeDtypeStruct((8, 128), f32),
         ),
-        in_specs=[hbm, vmem, smem, smem, smem, smem, smem, hbm, vmem],
-        out_specs=(vmem, vmem),
+        in_specs=[hbm] * 9,
+        out_specs=(hbm, hbm),
         scratch_shapes=[
+            pltpu.VMEM(control.shape, f32),
+            pltpu.SMEM(weights.shape, f32),
+            pltpu.SMEM(member_band.shape, member_band.dtype),
+            pltpu.SMEM(spread.shape, f32),
+            pltpu.SMEM(advect.shape, f32),
+            pltpu.SMEM(damping.shape, f32),
+            pltpu.VMEM(obs_weight.shape, f32),
+            pltpu.VMEM(control.shape, f32),
+            pltpu.VMEM((8, 128), f32),
+            dma((7,)),
+            dma((2,)),
             pltpu.VMEM((ml, vl) + field, ensemble.dtype),
             pltpu.VMEM((steps * 2 * planes,) + field, f32),
             pltpu.VMEM((ml,) + field, f32),
@@ -425,7 +457,7 @@
         + [dma((8,))] * 2
         + [dma((tiles - 1,))] * 2,
         compiler_params=pltpu.CompilerParams(
-            collective_id=0, has_side_effects=True, vmem_limit_bytes=60 * 1024 * 1024
+            collective_id=0, has_side_effects=True, vmem_limit_bytes=63 * 1024 * 1024
         ),
     )(ensemble, control, weights, member_band, spread, advect, damping, innovation, obs_weight)
     total_cells = tiles * rows * ny * vl

time: 58.5 us -> 55.5 us (0.949)
  Pallas kernels: 55 us -> 52 us
    pallas_call x1, Pallas kernels: 55 us -> 52 us  [per_device(): pl.pallas_call(functools.partial(kernel, n, tiles, steps, planes), out_sh...]
where the time goes in v3:
time: 55.5 us; the launch traced here: 55.2 us
  Pallas kernels  52 us (94%)
  local copies, waits for them, and re-layouts  1.32 us (2%)
  other arithmetic  1.3 us (2%)
  between operations  0.64 us (1%)
    pallas_call x1, Pallas kernels, per_device(): pl.pallas_call(functools.partial(kernel, n, tiles, steps, planes), out_sh...  52 us
    unnamed x1, local copies, waits for them, and re-layouts  1.32 us
    div x1, other arithmetic, per_device(): return (out, gw[:ml, 0] / math.sqrt(total_cells))  1.3 us

profile of v3, /device:TPU:0, one launch (start us, length us, event | category | flops | bytes accessed | tf_op | source)
XLA Modules:
  0.0 55.2 jit_solution(2947750546045523995)
XLA Ops:
  0.6 52.0 %shard_map.104 = (f32[2,8,256]{2,1,0:T(8,128)}, f32[8,128]{1,0:T(8,128)}) custom-call(bf16[2,256,8,256]{3,2,1,0:T(8,128)(2,1)} %ens.1, f32[2,8,256]{2,1,0:T(8,128)} %control_h.1, f32[2]{0:T(128)} %weights_h.1, s32[2]{0:T(128)} %band_h.1, f32[4]{0:T(128)} %spread_h.1, f32[2,256]{1,0:T(2,128)} %advect_h.1, f32[256]{0:T(256)} %damping_h.1, ...), custom_call_target="tpu_custom_call" | custom-call | tf_op jit(solution)/shard_map/pallas_call | solution.py:414
  52.6 1.3 %multiply_reduce_fusion = f32[2]{0:T(128)} fusion(f32[8,128]{1,0:T(8,128)} %get-tuple-element.5), kind=kLoop, calls=%fused_computation | loop fusion | flops 2 | bytes 16 | tf_op jit(solution)/shard_map/div | solution.py:464
  53.9 1.3 %copy.12 = f32[2,8,256]{2,1,0:T(8,128)} copy(f32[2,8,256]{2,1,0:T(8,128)} %get-tuple-element.8) | data formatting | bytes 32768
